TPU v7x, 32 devices: a whole 2x2x4 slice. The times are simulated.
32 devices in a mesh: aa: 8 (over z, x), ba: 4 (over y, core).
Axes of the slice: x: 2, y: 2, z: 4, core: 2. Of those that a mesh axis runs over, the one named last changes fastest.
Arguments:
- residual_a: bfloat16 [64, 4096], P('ba', 'aa'), may hold values from -160 to 160
- residual_b: bfloat16 [64, 3584], P(('aa', 'ba')), may hold values from -160 to 160
- encoder_a: bfloat16 [4096, 16384], P('ba', 'aa'), may hold values from -1 to 1
- bias_a: float32 [16384], P('aa'), may hold values from -12 to 12
- encoder_b: bfloat16 [3584, 16384], P('aa', 'ba'), may hold values from -1 to 1
- bias_b: float32 [16384], P('ba'), may hold values from -12 to 12
Outputs:
- match_score: float32 [16384, 16384], P('aa', 'ba')
- row_level: float32 [16384], P('aa')
- column_level: float32 [16384], P('ba')
All inputs are finite; a program needn't handle non-finite values.
Results may differ from a plain program's by a relative error of at most 0.0004.
The roundings to bfloat16 on the way count: a program that leaves them out, or rounds other values in their place, can miss the bound.
Values may be sent and summed in bfloat16 or wider, within the bound.
No kernel may reach another device: no remote copies, remote signals or barrier semaphores. Data moves between devices by JAX's collectives and lax.ppermute only.
A program may use at most 128 MiB of HBM per device.

v0:
```python
import jax
import jax.numpy as jnp
from jax import lax
from jax.sharding import PartitionSpec as P

INV_TEMP = 256
epsilon = 1e-05


def per_device(residual_a, residual_b, encoder_a, bias_a, encoder_b, bias_b):
    rows_a = lax.all_gather(residual_a, "aa", axis=1, tiled=True)
    inputs = rows_a
    encoded_a = jnp.dot(
        inputs,
        lax.all_gather(encoder_a, "ba", axis=0, tiled=True),
        preferred_element_type=jnp.float32,
    )
    fired_a = jnp.maximum(encoded_a + bias_a[None, :], 0.0)
    rows_b = lax.all_gather(residual_b, "ba", axis=0, tiled=True)
    columns_b = lax.all_to_all(rows_b, "aa", split_axis=1, concat_axis=0, tiled=True)
    inputs = columns_b
    encoded_b = lax.psum_scatter(
        jnp.dot(inputs, encoder_b, preferred_element_type=jnp.float32),
        "aa",
        scatter_dimension=0,
        tiled=True,
    )
    fired_b = jnp.maximum(encoded_b + bias_b[None, :], 0.0)
    token_total = float(rows_a.shape[0] * lax.axis_size("ba"))
    mean_a = lax.psum(jnp.sum(fired_a, 0), "ba") / token_total
    mean_b = lax.psum(jnp.sum(fired_b, 0), "aa") / token_total
    centered_a = fired_a - mean_a[None, :]
    centered_b = fired_b - mean_b[None, :]
    spread_a = lax.psum(jnp.sum(centered_a * centered_a, 0), "ba") / token_total
    spread_b = lax.psum(jnp.sum(centered_b * centered_b, 0), "aa") / token_total
    unit_a = (centered_a * lax.rsqrt(spread_a + epsilon)[None, :]).astype(jnp.bfloat16)
    unit_b = (centered_b * lax.rsqrt(spread_b + epsilon)[None, :]).astype(jnp.bfloat16)
    every_a = lax.all_gather(unit_a, "ba", axis=0, tiled=True)
    correlation = (
        lax.dot_general(
            every_a,
            lax.all_gather(unit_b, "aa", axis=0, tiled=True),
            (((0,), (0,)), ((), ())),
            preferred_element_type=jnp.float32,
        )
        / token_total
    )
    scores = correlation * INV_TEMP
    row_local = jnp.max(scores, axis=1)
    column_local = jnp.max(scores, axis=0)
    row_top = lax.pmax(row_local, "ba")
    column_top = lax.pmax(column_local, "aa")
    row_mass = lax.psum(jnp.sum(jnp.exp(scores - row_top[:, None]), axis=1), "ba")
    column_mass = lax.psum(jnp.sum(jnp.exp(scores - column_top[None, :]), axis=0), "aa")
    row_level = (row_top + jnp.log(row_mass)) / INV_TEMP
    column_level = (column_top + jnp.log(column_mass)) / INV_TEMP
    match_score = correlation - 0.5 * (row_level[:, None] + column_level[None, :])
    return (match_score, row_level, column_level)


def solution(mesh):
    return jax.shard_map(
        per_device,
        mesh=mesh,
        in_specs=(
            P("ba", "aa"),
            P(("aa", "ba"), None),
            P("ba", "aa"),
            P("aa"),
            P("aa", "ba"),
            P("ba"),
        ),
        out_specs=(P("aa", "ba"), P("aa"), P("ba")),
        check_vma=False,
    )
```

profile of v0, /device:TPU:0, one launch (start us, length us, event | category | flops | bytes accessed | tf_op | source)
XLA Modules:
  0.0 375.0 jit_solution(1914857120567517789)
XLA Ops:
  8.0 0.0 reduce-scatter.2.cloned.1.call-start
  8.0 6.5 %all-gather = bf16[4,2,3584]{2,1,0:T(2,128)(2,1)S(1)} all-gather(bf16[1,2,3584]{2,1,0:T(2,128)(2,1)} %bitcast.11), channel_id=1, replica_groups=mesh['aa'=8,'ba'=4] {'ba'}, dimensions={0}, use_global_device_ids=true | all-gather | bytes 71680 | tf_op jit(solution)/shard_map/all_gather | solution.py:19
  14.5 0.1 all_to_all.14
  14.7 12.9 %all_to_all.19 = bf16[8,8,448]{2,0,1:T(8,128)(2,1)S(1)} all-to-all(bf16[8,8,448]{2,0,1:T(8,128)(2,1)S(1)} %copy.10), channel_id=1, replica_groups=mesh['aa'=8,'ba'=4] {'aa'}, dimensions={1} | all-to-all | bytes 114688 | tf_op jit(solution)/shard_map/all_to_all | solution.py:20
  27.6 3.8 %fusion.2 = f32[64,4096]{1,0:T(8,128)} fusion(bf16[448,4096]{1,0:T(8,128)(2,1)} %param.10, bf16[8,8,448]{2,0,1:T(8,128)(2,1)S(1)} %all_to_all.19), kind=kOutput, calls=%fused_computation.13 | convolution fusion | flops 234881024 | bytes 4775936 | tf_op jit(solution)/shard_map/dot_general | solution.py:23
  31.4 0.0 reduce-scatter.2.cloned.1.call-update
  31.4 0.0 all-gather.3.cloned.1.call-start
  31.5 0.5 all-gather.3.cloned.1.call-update
  32.0 30.8 %all_gather.15 = bf16[16,4096]{1,0:T(8,128)(2,1)S(1)} all-gather(bf16[16,512]{1,0:T(8,128)(2,1)} %param.6), channel_id=1, replica_groups=mesh['aa'=8,'ba'=4] {'aa'}, dimensions={1}, use_global_device_ids=true | all-gather | bytes 147456 | tf_op jit(solution)/shard_map/all_gather | solution.py:11
  62.8 30.5 %reduce-scatter.2.cloned.1.call-done = f32[8,4096]{1,0:T(8,128)} async-done(((f32[64,4096]{1,0:T(8,128)}), f32[8,4096]{1,0:T(8,128)}) %reduce-scatter.2.cloned.1.call-update) | async-done | bytes 131088 | tf_op jit(solution)/shard_map/reduce_scatter | solution.py:22
  93.3 1.0 fusion.1
  94.3 35.0 %psum.44 = f32[4096]{0:T(1024)S(1)} all-reduce(f32[4096]{0:T(1024)S(1)} %fusion.1), channel_id=1, replica_groups=mesh['aa'=8,'ba'=4] {'aa'}, use_global_device_ids=true, to_apply=%region_6.0 | all-reduce | flops 4096 | bytes 32768 | tf_op jit(solution)/shard_map/psum | solution.py:31
  129.3 1.0 multiply_reduce_fusion.2
  130.3 33.0 %psum.45 = f32[4096]{0:T(1024)S(1)} all-reduce(f32[4096]{0:T(1024)S(1)} %multiply_reduce_fusion.2), channel_id=1, replica_groups=mesh['aa'=8,'ba'=4] {'aa'}, use_global_device_ids=true, to_apply=%region_8.0 | all-reduce | flops 4096 | bytes 32768 | tf_op jit(solution)/shard_map/psum | solution.py:35
  163.3 0.9 multiply_convert_fusion
  164.2 31.3 %all_gather.19 = bf16[64,4096]{1,0:T(8,128)(2,1)S(1)} all-gather(bf16[8,4096]{1,0:T(8,128)(2,1)S(1)} %multiply_convert_fusion), channel_id=1, replica_groups=mesh['aa'=8,'ba'=4] {'aa'}, dimensions={0}, use_global_device_ids=true | all-gather | bytes 589824 | tf_op jit(solution)/shard_map/all_gather | solution.py:42
  195.5 0.0 all-gather.3.cloned.1.call-done
  195.5 8.1 %fusion.4 = (f32[2048]{0:T(1024)S(1)}, f32[16,2048]{1,0:T(8,128)S(1)}) fusion(f32[2048]{0:T(1024)} %param.9, bf16[16,4096]{1,0:T(8,128)(2,1)S(1)} %all_gather.15, bf16[4096,2048]{1,0:T(8,128)(2,1)} %all-gather.3.cloned.1.call-done), kind=kOutput, calls=%fused_computation.21 | convolution fusion | flops 268531712 | bytes 17055744 | tf_op jit(solution)/shard_map/dot_general | solution.py:13
  203.6 5.8 %psum.42 = f32[2048]{0:T(1024)S(1)} all-reduce(f32[2048]{0:T(1024)S(1)} %get-tuple-element.5), channel_id=1, replica_groups=mesh['aa'=8,'ba'=4] {'ba'}, use_global_device_ids=true, to_apply=%region_1.0 | all-reduce | flops 2048 | bytes 16384 | tf_op jit(solution)/shard_map/psum | solution.py:30
  209.4 6.7 %psum.43 = f32[2048]{0:T(1024)S(1)} all-reduce(f32[2048]{0:T(1024)S(1)} %multiply_reduce_fusion.3), channel_id=1, replica_groups=mesh['aa'=8,'ba'=4] {'ba'}, use_global_device_ids=true, to_apply=%region_3.0 | all-reduce | flops 2048 | bytes 16384 | tf_op jit(solution)/shard_map/psum | solution.py:34
  216.1 5.8 %all_gather.17 = bf16[64,2048]{1,0:T(8,128)(2,1)S(1)} all-gather(bf16[16,2048]{1,0:T(8,128)(2,1)S(1)} %multiply_convert_fusion.1), channel_id=1, replica_groups=mesh['aa'=8,'ba'=4] {'ba'}, dimensions={0}, use_global_device_ids=true | all-gather | bytes 327680 | tf_op jit(solution)/shard_map/all_gather | solution.py:38
  221.9 14.1 %multiply_reduce_fusion.1 = (f32[2048]{0:T(1024)S(1)}, f32[2048,4096]{1,0:T(8,128)}) fusion(bf16[64,2048]{1,0:T(8,128)(2,1)S(1)} %all_gather.17, bf16[64,4096]{1,0:T(8,128)(2,1)S(1)} %all_gather.19), kind=kOutput, calls=%fused_computation.4 | convolution fusion | flops 1090516992 | bytes 34349056 | tf_op jit(solution)/shard_map/dot_general | solution.py:40
  235.9 6.7 %pmax.14 = f32[2048]{0:T(1024)S(1)} all-reduce(f32[2048]{0:T(1024)S(1)} %get-tuple-element.7), channel_id=1, replica_groups=mesh['aa'=8,'ba'=4] {'ba'}, use_global_device_ids=true, to_apply=%region_10.0 | all-reduce | flops 2048 | bytes 16384 | tf_op jit(solution)/shard_map/pmax | solution.py:51
  242.6 15.1 %exponential_reduce_fusion.1 = (f32[2048]{0:T(1024)S(1)}, f32[4096]{0:T(1024)S(1)}) fusion(f32[2048,4096]{1,0:T(8,128)} %get-tuple-element.8, f32[2048]{0:T(1024)S(1)} %pmax.14), kind=kLoop, calls=%fused_computation.2 | loop fusion | flops 33548288 | bytes 33587200 | tf_op jit(solution)/shard_map/reduce_sum | solution.py:53
  257.8 5.8 %psum.46 = f32[2048]{0:T(1024)S(1)} all-reduce(f32[2048]{0:T(1024)S(1)} %get-tuple-element.3), channel_id=1, replica_groups=mesh['aa'=8,'ba'=4] {'ba'}, use_global_device_ids=true, to_apply=%region_12.0 | all-reduce | flops 2048 | bytes 16384 | tf_op jit(solution)/shard_map/psum | solution.py:53
  263.5 0.0 copy-start.1
  263.6 33.0 %pmax.15 = f32[4096]{0:T(1024)S(1)} all-reduce(f32[4096]{0:T(1024)S(1)} %get-tuple-element.4), channel_id=1, replica_groups=mesh['aa'=8,'ba'=4] {'aa'}, use_global_device_ids=true, to_apply=%region_14.0 | all-reduce | flops 4096 | bytes 32768 | tf_op jit(solution)/shard_map/pmax | solution.py:52
  296.5 13.7 %exponential_reduce_fusion = f32[4096]{0:T(1024)S(1)} fusion(f32[2048,4096]{1,0:T(8,128)} %get-tuple-element.8, f32[4096]{0:T(1024)S(1)} %pmax.15), kind=kLoop, calls=%fused_computation.1 | loop fusion | flops 25161728 | bytes 33587200 | tf_op jit(solution)/shard_map/reduce_sum | solution.py:54
  310.3 33.0 %psum.47 = f32[4096]{0:T(1024)S(1)} all-reduce(f32[4096]{0:T(1024)S(1)} %exponential_reduce_fusion), channel_id=1, replica_groups=mesh['aa'=8,'ba'=4] {'aa'}, use_global_device_ids=true, to_apply=%region_16.0 | all-reduce | flops 4096 | bytes 32768 | tf_op jit(solution)/shard_map/psum | solution.py:54
  343.3 0.0 copy-start
  343.3 24.3 %multiply_subtract_fusion = f32[2048,4096]{1,0:T(8,128)} fusion(f32[2048,4096]{1,0:T(8,128)} %get-tuple-element.8, f32[4096]{0:T(1024)S(1)} %add_multiply_fusion, f32[2048]{0:T(1024)S(1)} %add_multiply_fusion.1), kind=kLoop, calls=%fused_computation | loop fusion | flops 33554432 | bytes 67133440 | tf_op jit(solution)/shard_map/sub | solution.py:57
  367.5 0.0 copy-done.1
  367.6 0.0 copy-done
  (9 shorter events, 0.1 us)
Async XLA Ops:
  8.0 85.3 %reduce-scatter.2.cloned.1.call-start = ((), (), s32[]{:S(2)}) async-start(), calls=%async_computation.3 | async-start | bytes 1179648 | tf_op jit(solution)/shard_map/reduce_scatter | solution.py:22
  31.4 164.1 %all-gather.3.cloned.1.call-start = ((), (), s32[]{:S(2)}) async-start(), calls=%async_computation.2 | async-start | bytes 20971520 | tf_op jit(solution)/shard_map/all_gather | solution.py:15
  263.5 104.0 %copy-start.1 = (f32[2048]{0:T(1024)}, f32[2048]{0:T(1024)S(1)}, u32[]{:S(2)}) copy-start(f32[2048]{0:T(1024)S(1)} %add_multiply_fusion.1) | copy-start | bytes 24580
  343.3 24.3 %copy-start = (f32[4096]{0:T(1024)}, f32[4096]{0:T(1024)S(1)}, u32[]{:S(2)}) copy-start(f32[4096]{0:T(1024)S(1)} %add_multiply_fusion) | copy-start | bytes 49156
Sparse Core Ops, SparseCore 0:
  31.5 61.7 reduce-scatter.1
Sparse Core Ops, SparseCore 1:
  33.5 103.3 all-gather.2
where the time goes:
time: 376 us; the launch traced here: 375 us
  blocking collectives  246 us (65%)
  other arithmetic  56.1 us (15%)
  waiting for transfers between devices  31.1 us (8%)
  matrix products  25.9 us (7%)
  between operations  15.6 us (4%)
    psum x1, blocking collectives, per_device(): mean_b = lax.psum(jnp.sum(fired_b, 0), 'aa') / token_total  35 us
    psum x1, blocking collectives, per_device(): spread_b = lax.psum(jnp.sum(centered_b * centered_b, 0), 'aa') / token_total  33 us
    pmax x1, blocking collectives, per_device(): column_top = lax.pmax(column_local, 'aa')  33 us
    psum x1, blocking collectives, per_device(): lax.psum(jnp.sum(jnp.exp(scores - column_top[None, :]), axis=0), 'aa')  33 us
    all_gather x1, blocking collectives, per_device(): lax.all_gather(unit_b, 'aa', axis=0, tiled=True)  31.3 us
    all_gather x1, blocking collectives, per_device(): rows_a = lax.all_gather(residual_a, 'aa', axis=1, tiled=True)  30.8 us
    reduce_scatter x1, waiting for transfers between devices, per_device(): lax.psum_scatter(jnp.dot(inputs, encoder_b, preferred_element_type=jnp.fl...  30.5 us
    sub x1, other arithmetic, per_device(): correlation - 0.5 * (row_level[:, None] + column_level[None, :])  24.3 us
  transfers between devices with their start and end apart: 2, of which 1 were waited for; matrix products, arithmetic and copies ran while one was open for 1% of the time, Pallas kernels for 0%

commit v1 on v0

--- a/solution.py
+++ b/solution.py
@@ -36,10 +36,19 @@
     unit_a = (centered_a * lax.rsqrt(spread_a + epsilon)[None, :]).astype(jnp.bfloat16)
     unit_b = (centered_b * lax.rsqrt(spread_b + epsilon)[None, :]).astype(jnp.bfloat16)
     every_a = lax.all_gather(unit_a, "ba", axis=0, tiled=True)
+    ladders_hold = lambda x_in, dev_axis: jnp.concatenate(
+        jax.lax.all_to_all(
+            jnp.stack([x_in] * jax.lax.axis_size(dev_axis), 0),
+            axis_name=dev_axis,
+            split_axis=0,
+            concat_axis=0,
+        ),
+        0,
+    )
     correlation = (
         lax.dot_general(
             every_a,
-            lax.all_gather(unit_b, "aa", axis=0, tiled=True),
+            ladders_hold(unit_b, "aa"),
             (((0,), (0,)), ((), ())),
             preferred_element_type=jnp.float32,
         )

time: 376 us -> 353 us (0.939)
  blocking collectives: 246 us -> 219 us
    all_gather x1 -> x0, blocking collectives: 31.3 us -> none  [per_device(): lax.all_gather(unit_b, 'aa', axis=0, tiled=True)]
    pmax x1, blocking collectives: 33 us -> 37.5 us  [per_device(): column_top = lax.pmax(column_local, 'aa')]
  transfers between devices with their start and end apart: 2 -> 3, of which waited for: 1 -> 1; matrix products, arithmetic and copies ran while one was open for 1% -> 3% of each run, Pallas kernels for 0% -> 0%
where the time goes in v1:
time: 353 us
  blocking collectives  219 us (62%)
  other arithmetic  56.1 us (16%)
  waiting for transfers between devices  31.1 us (9%)
  matrix products  25.9 us (7%)
  between operations  15.6 us (4%)
  starting transfers between devices  3.58 us (1%)
    pmax x1, blocking collectives, per_device(): column_top = lax.pmax(column_local, 'aa')  37.5 us
    psum x1, blocking collectives, per_device(): mean_b = lax.psum(jnp.sum(fired_b, 0), 'aa') / token_total  35 us
    psum x1, blocking collectives, per_device(): spread_b = lax.psum(jnp.sum(centered_b * centered_b, 0), 'aa') / token_total  33 us
    psum x1, blocking collectives, per_device(): lax.psum(jnp.sum(jnp.exp(scores - column_top[None, :]), axis=0), 'aa')  33 us
    all_gather x1, blocking collectives, per_device(): rows_a = lax.all_gather(residual_a, 'aa', axis=1, tiled=True)  30.8 us
    reduce_scatter x1, waiting for transfers between devices, per_device(): lax.psum_scatter(jnp.dot(inputs, encoder_b, preferred_element_type=jnp.fl...  30.5 us
    sub x1, other arithmetic, per_device(): correlation - 0.5 * (row_level[:, None] + column_level[None, :])  24.3 us
    reduce_sum x1, other arithmetic, per_device(): jnp.sum(jnp.exp(scores - row_top[:, None]), axis=1)  15.1 us
  transfers between devices with their start and end apart: 3, of which 1 were waited for; matrix products, arithmetic and copies ran while one was open for 3% of the time, Pallas kernels for 0%

profile of v1, /device:TPU:0, one launch (start us, length us, event | category | flops | bytes accessed | tf_op | source)
XLA Modules:
  0.0 352.6 jit_solution(16537722093834766318)
XLA Ops:
  8.0 0.0 reduce-scatter.2.cloned.1.call-start
  8.0 6.5 %all-gather = bf16[4,2,3584]{2,1,0:T(2,128)(2,1)S(1)} all-gather(bf16[1,2,3584]{2,1,0:T(2,128)(2,1)} %bitcast.15), channel_id=1, replica_groups=mesh['aa'=8,'ba'=4] {'ba'}, dimensions={0}, use_global_device_ids=true | all-gather | bytes 71680 | tf_op jit(solution)/shard_map/all_gather | solution.py:19
  14.5 0.1 all_to_all.17
  14.7 12.9 %all_to_all.24 = bf16[8,8,448]{2,0,1:T(8,128)(2,1)S(1)} all-to-all(bf16[8,8,448]{2,0,1:T(8,128)(2,1)S(1)} %copy.10), channel_id=1, replica_groups=mesh['aa'=8,'ba'=4] {'aa'}, dimensions={1} | all-to-all | bytes 114688 | tf_op jit(solution)/shard_map/all_to_all | solution.py:20
  27.6 3.8 %fusion.4 = f32[64,4096]{1,0:T(8,128)} fusion(bf16[448,4096]{1,0:T(8,128)(2,1)} %param.10, bf16[8,8,448]{2,0,1:T(8,128)(2,1)S(1)} %all_to_all.24), kind=kOutput, calls=%fused_computation.15 | convolution fusion | flops 234881024 | bytes 4775936 | tf_op jit(solution)/shard_map/dot_general | solution.py:23
  31.4 0.0 reduce-scatter.2.cloned.1.call-update
  31.4 0.0 all-gather.3.cloned.1.call-start
  31.5 0.5 all-gather.3.cloned.1.call-update
  32.0 30.8 %all_gather.12 = bf16[16,4096]{1,0:T(8,128)(2,1)S(1)} all-gather(bf16[16,512]{1,0:T(8,128)(2,1)} %param.6), channel_id=1, replica_groups=mesh['aa'=8,'ba'=4] {'aa'}, dimensions={1}, use_global_device_ids=true | all-gather | bytes 147456 | tf_op jit(solution)/shard_map/all_gather | solution.py:11
  62.8 30.5 %reduce-scatter.2.cloned.1.call-done = f32[8,4096]{1,0:T(8,128)} async-done(((f32[64,4096]{1,0:T(8,128)}), f32[8,4096]{1,0:T(8,128)}) %reduce-scatter.2.cloned.1.call-update) | async-done | bytes 131088 | tf_op jit(solution)/shard_map/reduce_scatter | solution.py:22
  93.3 1.0 fusion.3
  94.3 35.0 %psum.44 = f32[4096]{0:T(1024)S(1)} all-reduce(f32[4096]{0:T(1024)S(1)} %fusion.3), channel_id=1, replica_groups=mesh['aa'=8,'ba'=4] {'aa'}, use_global_device_ids=true, to_apply=%region_6.0 | all-reduce | flops 4096 | bytes 32768 | tf_op jit(solution)/shard_map/psum | solution.py:31
  129.3 1.0 multiply_reduce_fusion.2
  130.3 33.0 %psum.45 = f32[4096]{0:T(1024)S(1)} all-reduce(f32[4096]{0:T(1024)S(1)} %multiply_reduce_fusion.2), channel_id=1, replica_groups=mesh['aa'=8,'ba'=4] {'aa'}, use_global_device_ids=true, to_apply=%region_8.0 | all-reduce | flops 4096 | bytes 32768 | tf_op jit(solution)/shard_map/psum | solution.py:35
  163.3 0.9 multiply_convert_fusion
  164.2 0.8 stack.2
  165.1 3.5 all-to-all-start.1
  168.6 0.0 all-gather.3.cloned.1.call-done
  168.6 8.1 %fusion.6 = (f32[2048]{0:T(1024)S(1)}, f32[16,2048]{1,0:T(8,128)S(1)}) fusion(f32[2048]{0:T(1024)} %param.9, bf16[16,4096]{1,0:T(8,128)(2,1)S(1)} %all_gather.12, bf16[4096,2048]{1,0:T(8,128)(2,1)} %all-gather.3.cloned.1.call-done), kind=kOutput, calls=%fused_computation.23 | convolution fusion | flops 268531712 | bytes 17055744 | tf_op jit(solution)/shard_map/dot_general | solution.py:13
  176.7 5.8 %psum.42 = f32[2048]{0:T(1024)S(1)} all-reduce(f32[2048]{0:T(1024)S(1)} %get-tuple-element.5), channel_id=1, replica_groups=mesh['aa'=8,'ba'=4] {'ba'}, use_global_device_ids=true, to_apply=%region_1.0 | all-reduce | flops 2048 | bytes 16384 | tf_op jit(solution)/shard_map/psum | solution.py:30
  182.5 6.7 %psum.43 = f32[2048]{0:T(1024)S(1)} all-reduce(f32[2048]{0:T(1024)S(1)} %multiply_reduce_fusion.3), channel_id=1, replica_groups=mesh['aa'=8,'ba'=4] {'ba'}, use_global_device_ids=true, to_apply=%region_3.0 | all-reduce | flops 2048 | bytes 16384 | tf_op jit(solution)/shard_map/psum | solution.py:34
  189.2 5.8 %all_gather.14 = bf16[64,2048]{1,0:T(8,128)(2,1)S(1)} all-gather(bf16[16,2048]{1,0:T(8,128)(2,1)S(1)} %multiply_convert_fusion.1), channel_id=1, replica_groups=mesh['aa'=8,'ba'=4] {'ba'}, dimensions={0}, use_global_device_ids=true | all-gather | bytes 327680 | tf_op jit(solution)/shard_map/all_gather | solution.py:38
  195.0 0.0 all-to-all-done.1
  195.0 14.1 %multiply_reduce_fusion.1 = (f32[2048]{0:T(1024)S(1)}, f32[2048,4096]{1,0:T(8,128)}) fusion(bf16[64,2048]{1,0:T(8,128)(2,1)S(1)} %all_gather.14, bf16[8,8,4096]{2,1,0:T(8,128)(2,1)S(1)} %all-to-all-done.1), kind=kOutput, calls=%fused_computation.4 | convolution fusion | flops 1090516992 | bytes 34349056 | tf_op jit(solution)/shard_map/dot_general | solution.py:49
  209.0 6.7 %pmax.14 = f32[2048]{0:T(1024)S(1)} all-reduce(f32[2048]{0:T(1024)S(1)} %get-tuple-element.7), channel_id=1, replica_groups=mesh['aa'=8,'ba'=4] {'ba'}, use_global_device_ids=true, to_apply=%region_10.0 | all-reduce | flops 2048 | bytes 16384 | tf_op jit(solution)/shard_map/pmax | solution.py:60
  215.7 15.1 %exponential_reduce_fusion.1 = (f32[2048]{0:T(1024)S(1)}, f32[4096]{0:T(1024)S(1)}) fusion(f32[2048,4096]{1,0:T(8,128)} %get-tuple-element.8, f32[2048]{0:T(1024)S(1)} %pmax.14), kind=kLoop, calls=%fused_computation.2 | loop fusion | flops 33548288 | bytes 33587200 | tf_op jit(solution)/shard_map/reduce_sum | solution.py:62
  230.9 5.8 %psum.46 = f32[2048]{0:T(1024)S(1)} all-reduce(f32[2048]{0:T(1024)S(1)} %get-tuple-element.3), channel_id=1, replica_groups=mesh['aa'=8,'ba'=4] {'ba'}, use_global_device_ids=true, to_apply=%region_12.0 | all-reduce | flops 2048 | bytes 16384 | tf_op jit(solution)/shard_map/psum | solution.py:62
  236.7 0.0 copy-start.1
  236.7 37.5 %pmax.15 = f32[4096]{0:T(1024)S(1)} all-reduce(f32[4096]{0:T(1024)S(1)} %get-tuple-element.4), channel_id=1, replica_groups=mesh['aa'=8,'ba'=4] {'aa'}, use_global_device_ids=true, to_apply=%region_14.0 | all-reduce | flops 4096 | bytes 32768 | tf_op jit(solution)/shard_map/pmax | solution.py:61
  274.1 13.7 %exponential_reduce_fusion = f32[4096]{0:T(1024)S(1)} fusion(f32[2048,4096]{1,0:T(8,128)} %get-tuple-element.8, f32[4096]{0:T(1024)S(1)} %pmax.15), kind=kLoop, calls=%fused_computation.1 | loop fusion | flops 25161728 | bytes 33587200 | tf_op jit(solution)/shard_map/reduce_sum | solution.py:63
  287.9 33.0 %psum.47 = f32[4096]{0:T(1024)S(1)} all-reduce(f32[4096]{0:T(1024)S(1)} %exponential_reduce_fusion), channel_id=1, replica_groups=mesh['aa'=8,'ba'=4] {'aa'}, use_global_device_ids=true, to_apply=%region_16.0 | all-reduce | flops 4096 | bytes 32768 | tf_op jit(solution)/shard_map/psum | solution.py:63
  320.9 0.0 copy-start
  320.9 24.3 %multiply_subtract_fusion = f32[2048,4096]{1,0:T(8,128)} fusion(f32[2048,4096]{1,0:T(8,128)} %get-tuple-element.8, f32[4096]{0:T(1024)S(1)} %add_multiply_fusion, f32[2048]{0:T(1024)S(1)} %add_multiply_fusion.1), kind=kLoop, calls=%fused_computation | loop fusion | flops 33554432 | bytes 67133440 | tf_op jit(solution)/shard_map/sub | solution.py:66
  345.1 0.0 copy-done.1
  345.1 0.0 copy-done
  (9 shorter events, 0.1 us)
Async XLA Ops:
  8.0 85.3 %reduce-scatter.2.cloned.1.call-start = ((), (), s32[]{:S(2)}) async-start(), calls=%async_computation.4 | async-start | bytes 1179648 | tf_op jit(solution)/shard_map/reduce_scatter | solution.py:22
  31.4 137.2 %all-gather.3.cloned.1.call-start = ((), (), s32[]{:S(2)}) async-start(), calls=%async_computation.3 | async-start | bytes 20971520 | tf_op jit(solution)/shard_map/all_gather | solution.py:15
  165.1 29.9 %all-to-all-start.1 = ((bf16[8,8,4096]{2,1,0:T(8,128)(2,1)}), bf16[8,8,4096]{2,1,0:T(8,128)(2,1)S(1)}, u32[]{:S(2)}, u32[]{:S(2)}) async-start(bf16[8,8,4096]{2,1,0:T(8,128)(2,1)} %stack.2), calls=%async_computation.2 | async-start | bytes 1048576 | tf_op jit(solution)/shard_map/all_to_all | solution.py:40
  236.7 108.5 %copy-start.1 = (f32[2048]{0:T(1024)}, f32[2048]{0:T(1024)S(1)}, u32[]{:S(2)}) copy-start(f32[2048]{0:T(1024)S(1)} %add_multiply_fusion.1) | copy-start | bytes 24580
  320.9 24.3 %copy-start = (f32[4096]{0:T(1024)}, f32[4096]{0:T(1024)S(1)}, u32[]{:S(2)}) copy-start(f32[4096]{0:T(1024)S(1)} %add_multiply_fusion) | copy-start | bytes 49156
Sparse Core Ops, SparseCore 0:
  31.5 61.7 reduce-scatter.1
Sparse Core Ops, SparseCore 1:
  33.5 103.3 all-gather.2
